TPU v7x, 32 devices: a whole 2x2x4 slice. The times are simulated.
32 devices in a mesh: dp: 8 (over z, y), tensor: 4 (over x, core).
Axes of the slice: x: 2, y: 2, z: 4, core: 2. Of those that a mesh axis runs over, the one named last changes fastest.
Arguments:
- hidden: bfloat16 [128, 4096], P(('dp', 'tensor')), may hold values from -6 to 6
- shortcut: bfloat16 [128, 4096], P('dp'), may hold values from -6 to 6
- expert_ids: int32 [128, 2], P('dp'), may hold values from 0 to 7, all different within a row; in each aligned block of 16 rows (0 to 15, 16 to 31, ...) at most 6 rows name the same one
- route_weight: float32 [128, 2], P('dp'), may hold values from 0.1 to 1
- dense_gain: float32 [4096], replicated, may hold values from 0.5 to 1.5
- moe_gain: float32 [4096], replicated, may hold values from 0.5 to 1.5
- dense_gate: bfloat16 [4096, 8192], P(None, 'dp'), may hold values from -0.09375 to 0.09375
- dense_lift: bfloat16 [4096, 8192], P(None, 'dp'), may hold values from -0.09375 to 0.09375
- dense_down: bfloat16 [8192, 4096], P('dp'), may hold values from -0.0625 to 0.0625
- expert_gate: bfloat16 [4096, 65536], P(None, ('dp', 'tensor')), may hold values from -0.09375 to 0.09375
- expert_lift: bfloat16 [4096, 65536], P(None, ('dp', 'tensor')), may hold values from -0.09375 to 0.09375
- expert_down: bfloat16 [65536, 4096], P(('dp', 'tensor')), may hold values from -0.0625 to 0.0625
Outputs:
- mixed: bfloat16 [128, 4096], P(('dp', 'tensor'))
Inputs may be any that keep to these rules, and one draw needn't show every extreme that they name: `expert_ids`: the 2 experts of a token differ. In each aligned block of 16 rows (the tokens of one index of dp) no expert is named by more than 6 rows, and in every draw some expert is named by exactly 6 rows of some block; every expert is named somewhere.
All inputs are finite; a program needn't handle non-finite values.
Results may differ from a plain program's by a relative error of at most 0.006.
Values may be sent and summed in bfloat16 or wider, within the bound.
A program may use at most 128 MiB of HBM per device.

v0:
```python
import jax
import jax.numpy as jnp
from jax import lax
from jax.sharding import PartitionSpec as P

D = 4096
E = 8
TOP = 2
CAP = 6


EPSILON = 1e-05


def normalize(values_in, gain):
    values = values_in.astype(jnp.float32)
    scale = lax.rsqrt(jnp.mean(values * values, axis=-1, keepdims=True) + EPSILON)
    return (values * scale * gain).astype(jnp.bfloat16)


def local(
    hidden,
    shortcut,
    expert_ids,
    route_weight,
    dense_gain,
    moe_gain,
    dense_gate,
    dense_lift,
    dense_down,
    expert_gate,
    expert_lift,
    expert_down,
):
    normed = normalize(hidden, dense_gain)
    piece = lax.all_gather(normed, "dp", axis=0, tiled=True)
    gate_vals = jnp.dot(piece, dense_gate, preferred_element_type=jnp.float32)
    lift_vals = jnp.dot(piece, dense_lift, preferred_element_type=jnp.float32)
    dense_inner = (jax.nn.silu(gate_vals) * lift_vals).astype(jnp.bfloat16)
    dense_out = lax.psum_scatter(
        jnp.dot(dense_inner, dense_down, preferred_element_type=jnp.float32),
        "dp",
        scatter_dimension=0,
        tiled=True,
    )
    members = lax.axis_size("dp") // E
    token_count = shortcut.shape[0]
    moe_in = normalize(shortcut, moe_gain)
    flat = expert_ids.reshape(token_count * TOP)
    picked = (flat[:, None] == jnp.arange(E, dtype=jnp.int32)[None, :]).astype(jnp.int32)
    before = jnp.cumsum(picked, axis=0) - picked
    places = flat * CAP + jnp.sum(before * picked, axis=1)
    chosen = (places[:, None] == jnp.arange(E * CAP, dtype=jnp.int32)[None, :]).astype(jnp.float32)
    chosen = chosen.reshape(token_count, TOP, E * CAP)
    spread = jnp.sum(chosen, axis=1).astype(jnp.bfloat16)
    weighted = jnp.sum(chosen * route_weight[:, :, None], axis=1)
    buffer = lax.dot_general(
        spread, moe_in, (((0,), (0,)), ((), ())), preferred_element_type=jnp.float32
    )
    buffer = buffer.astype(jnp.bfloat16).reshape(E, CAP, D)
    outgoing = jnp.repeat(buffer, members, axis=0)
    arrived = lax.all_to_all(outgoing, "dp", split_axis=0, concat_axis=0, tiled=True)
    sources, count, width = arrived.shape
    rows_in = arrived.reshape(sources * count, width)
    gate_vals = jnp.dot(rows_in, expert_gate, preferred_element_type=jnp.float32)
    lift_vals = jnp.dot(rows_in, expert_lift, preferred_element_type=jnp.float32)
    inner = (jax.nn.silu(gate_vals) * lift_vals).astype(jnp.bfloat16)
    terms = jnp.dot(inner, expert_down, preferred_element_type=jnp.float32).astype(jnp.bfloat16)
    returned = lax.all_to_all(
        terms.reshape(sources, count, D), "dp", split_axis=0, concat_axis=0, tiled=True
    )
    summed = jnp.sum(returned.astype(jnp.float32).reshape(E, members, CAP, D), axis=1).reshape(
        E * CAP, D
    )
    moe_part = jnp.dot(
        weighted, summed, precision=lax.Precision.HIGHEST, preferred_element_type=jnp.float32
    )
    moe_out = lax.psum_scatter(moe_part, "tensor", scatter_dimension=0, tiled=True)
    return (hidden.astype(jnp.float32) + dense_out + moe_out).astype(jnp.bfloat16)


def solution(mesh):
    in_specs = (
        P(("dp", "tensor"), None),
        P("dp", None),
        P("dp", None),
        P("dp", None),
        P(),
        P(),
        P(None, "dp"),
        P(None, "dp"),
        P("dp", None),
        P(None, ("dp", "tensor")),
        P(None, ("dp", "tensor")),
        P(("dp", "tensor"), None),
    )
    out_specs = P(("dp", "tensor"), None)
    return jax.shard_map(local, mesh=mesh, in_specs=in_specs, out_specs=out_specs, check_vma=False)
```

profile of v0, /device:TPU:0, one launch (start us, length us, event | category | flops | bytes accessed | tf_op | source)
XLA Modules:
  0.0 215.8 jit_solution(18423160063778586891)
XLA Ops:
  6.5 0.8 copy.29
  7.5 0.2 select_reduce_fusion.1
  7.9 0.7 multiply_add_fusion
  8.6 1.0 fusion.8
  9.6 0.8 convert_reduce_fusion
  10.4 1.2 convolution_convert_fusion.1
  11.6 0.9 reshape_broadcast_in_dim_reshape.3
  12.5 7.3 %all-to-all-start = ((bf16[8,6,4096]{2,1,0:T(8,128)(2,1)}), bf16[8,6,4096]{2,1,0:T(8,128)(2,1)S(1)}, u32[]{:S(2)}, u32[]{:S(2)}) async-start(bf16[8,6,4096]{2,1,0:T(8,128)(2,1)} %reshape_broadcast_in_dim_reshape.3), calls=%async_computation | async-start | bytes 1048576 | tf_op jit(solution)/shard_map/all_to_all | solution.py:62
  19.8 0.9 fusion.20
  20.8 0.9 fusion.26
  21.6 36.0 %all-gather = bf16[8,4,4096]{2,1,0:T(4,128)(2,1)S(1)} all-gather(bf16[1,4,4096]{2,1,0:T(4,128)(2,1)S(1)} %fusion.26), channel_id=1, replica_groups=mesh['dp'=8,'tensor'=4] {'dp'}, dimensions={0}, use_global_device_ids=true | all-gather | bytes 294912 | tf_op jit(solution)/shard_map/all_gather | solution.py:36
  57.7 4.9 %fusion.31 = f32[32,1024]{1,0:T(8,128)S(1)} fusion(bf16[32,4096]{1,0:T(8,128)(2,1)S(1)} %reshape.55, bf16[4096,1024]{1,0:T(8,128)(2,1)} %param.18), kind=kOutput, calls=%fused_computation.47 | convolution fusion | flops 268435456 | bytes 8781824 | tf_op jit(solution)/shard_map/dot_general | solution.py:37
  62.8 8.8 %fusion.32 = f32[48,2048]{1,0:T(8,128)S(1)} fusion(bf16[48,4096]{1,0:T(8,128)(2,1)S(1)} %reshape.51, bf16[4096,2048]{1,0:T(8,128)(2,1)} %param.21), kind=kOutput, calls=%fused_computation.48 | convolution fusion | flops 805306368 | bytes 17563648 | tf_op jit(solution)/shard_map/dot_general | solution.py:65
  71.5 13.7 %convolution_convert_fusion = bf16[48,4096]{1,0:T(8,128)(2,1)S(1)} fusion(bf16[2048,4096]{1,0:T(8,128)(2,1)} %param.23, bf16[48,4096]{1,0:T(8,128)(2,1)S(1)} %reshape.51, bf16[4096,2048]{1,0:T(8,128)(2,1)} %param.22, f32[48,2048]{1,0:T(8,128)S(1)} %fusion.32), kind=kOutput, calls=%fused_computation | convolution fusion | flops 1611399168 | bytes 34734080 | tf_op jit(solution)/shard_map/dot_general | solution.py:68
  85.3 1.0 reshape.52
  86.2 3.5 %all-to-all-start.1 = ((bf16[8,6,4096]{2,1,0:T(8,128)(2,1)}), bf16[8,6,4096]{2,1,0:T(8,128)(2,1)S(1)}, u32[]{:S(2)}, u32[]{:S(2)}) async-start(bf16[8,6,4096]{2,1,0:T(8,128)(2,1)} %reshape.52), calls=%async_computation.1 | async-start | bytes 1048576 | tf_op jit(solution)/shard_map/all_to_all | solution.py:69
  89.8 9.6 %fusion.2 = f32[32,4096]{1,0:T(8,128)} fusion(bf16[1024,4096]{1,0:T(8,128)(2,1)} %param.20, bf16[32,4096]{1,0:T(8,128)(2,1)S(1)} %reshape.55, bf16[4096,1024]{1,0:T(8,128)(2,1)} %param.19, f32[32,1024]{1,0:T(8,128)S(1)} %fusion.31), kind=kOutput, calls=%fused_computation.6 | convolution fusion | flops 537067520 | bytes 17694720 | tf_op jit(solution)/shard_map/dot_general | solution.py:41
  99.4 0.5 all-to-all-done.1
  100.1 1.0 fusion.33
  101.1 0.6 dynamic-slice
  101.7 0.6 dynamic-slice.2
  103.6 70.0 %all-reduce.5.cloned.1.call-done = f32[32,4096]{1,0:T(8,128)} async-done(((f32[32,4096]{1,0:T(8,128)}), f32[32,4096]{1,0:T(8,128)}) %all-reduce.5.cloned.1.call-update) | async-done | bytes 524304
  173.6 33.8 %all-reduce.7.cloned.1.call-done = f32[16,4096]{1,0:T(8,128)} async-done(((f32[16,4096]{1,0:T(8,128)}), f32[16,4096]{1,0:T(8,128)}) %all-reduce.7.cloned.1.call-update) | async-done | bytes 262160
  207.4 1.6 fusion.24
  (21 shorter events, 0.9 us)
Async XLA Ops:
  12.5 50.1 %all-to-all-start = ((bf16[8,6,4096]{2,1,0:T(8,128)(2,1)}), bf16[8,6,4096]{2,1,0:T(8,128)(2,1)S(1)}, u32[]{:S(2)}, u32[]{:S(2)}) async-start(bf16[8,6,4096]{2,1,0:T(8,128)(2,1)} %reshape_broadcast_in_dim_reshape.3), calls=%async_computation | async-start | bytes 1048576 | tf_op jit(solution)/shard_map/all_to_all | solution.py:62
  85.2 15.9 %copy-start.2 = (u32[32]{0:T(128)S(1)}, u32[32]{0:T(128)}, u32[]{:S(2)}) copy-start(u32[32]{0:T(128)} %constant.27) | copy-start | bytes 388
  85.2 16.5 %copy-start.1 = (u32[32]{0:T(128)S(1)}, u32[32]{0:T(128)}, u32[]{:S(2)}) copy-start(u32[32]{0:T(128)} %constant.31) | copy-start | bytes 388
  85.2 122.1 %copy-start = (bf16[4,4096]{1,0:T(4,128)(2,1)S(1)}, bf16[4,4096]{1,0:T(4,128)(2,1)}, u32[]{:S(2)}) copy-start(bf16[4,4096]{1,0:T(4,128)(2,1)} %param.12) | copy-start | bytes 98308
  86.2 13.7 %all-to-all-start.1 = ((bf16[8,6,4096]{2,1,0:T(8,128)(2,1)}), bf16[8,6,4096]{2,1,0:T(8,128)(2,1)S(1)}, u32[]{:S(2)}, u32[]{:S(2)}) async-start(bf16[8,6,4096]{2,1,0:T(8,128)(2,1)} %reshape.52), calls=%async_computation.1 | async-start | bytes 1048576 | tf_op jit(solution)/shard_map/all_to_all | solution.py:69
  89.7 83.8 %all-reduce.5.cloned.1.call-start = ((), (), s32[]{:S(2)}) async-start(), calls=%async_computation.2 | async-start | bytes 1048576
  99.4 108.0 %all-reduce.7.cloned.1.call-start = ((), (), s32[]{:S(2)}) async-start(), calls=%async_computation.3 | async-start | bytes 524288
Sparse Core Ops, SparseCore 0:
  99.5 73.9 all-reduce.4
  175.9 31.4 all-reduce.6
where the time goes:
time: 216 us
  waiting for transfers between devices  104 us (48%)
  matrix products  39.2 us (18%)
  blocking collectives  36 us (17%)
  between operations  14.8 us (7%)
  starting transfers between devices  10.9 us (5%)
  other arithmetic  6.21 us (3%)
  local copies, waits for them, and re-layouts  4.44 us (2%)
    unnamed x4, waiting for transfers between devices  104 us
    all_gather x1, blocking collectives, local(): piece = lax.all_gather(normed, 'dp', axis=0, tiled=True)  36 us
    dot_general x1, matrix products, local(): jnp.dot(inner, expert_down, preferred_element_type=jnp.float32)  13.7 us
    dot_general x1, matrix products, local(): jnp.dot(dense_inner, dense_down, preferred_element_type=jnp.float32)  9.6 us
    dot_general x1, matrix products, local(): jnp.dot(rows_in, expert_gate, preferred_element_type=jnp.float32)  8.79 us
    all_to_all x1, starting transfers between devices, local(): lax.all_to_all(outgoing, 'dp', split_axis=0, concat_axis=0, tiled=True)  7.31 us
    dot_general x1, matrix products, local(): gate_vals = jnp.dot(piece, dense_gate, preferred_element_type=jnp.float32)  4.92 us
  transfers between devices with their start and end apart: 4, of which 3 were waited for; matrix products, arithmetic and copies ran while one was open for 9% of the time, Pallas kernels for 0%

commit v1 on v0

v1 whole, which is shorter than its diff:
```python
import functools

import jax
import jax.numpy as jnp
from jax import lax
from jax.experimental import pallas as pl
from jax.experimental.pallas import tpu as pltpu
from jax.sharding import PartitionSpec as P

E = 8
TOP = 2
CAP = 6
CP = 8
EPSILON = 1e-05
MESH = pl.DeviceIdType.MESH
F32 = jnp.float32
BF16 = jnp.bfloat16


def rms_scale(values):
    return lax.rsqrt(jnp.mean(values * values, axis=-1, keepdims=True) + EPSILON)


def gated(rows, gate, lift):
    g = jnp.dot(rows, gate, preferred_element_type=F32)
    v = jnp.dot(rows, lift, preferred_element_type=F32)
    return (g / (1.0 + jnp.exp(-g)) * v).astype(BF16)


def kernel(
    cfg,
    hidden, shortcut, ids, route, dgain, mgain, dg, dl, dd, eg, el, ed,
    out,
    gpool, lpool, dpool, epool,
    ag, stage, xd, inner_d, ds, dland,
    disp, land, xe, inner_e, rs, rsland, ret, retland, fin, finland,
    gsem, lsem, dsem, esem,
    ag_s, ag_r, di_s, di_r, rl_s, rl_r, ds_s, ds_r, rs_s, rs_r, re_s, re_r, fi_s, fi_r,
):
    np_, nt, cw, ns, nd, ne, dc, ec = cfg
    h, D = hidden.shape
    B = shortcut.shape[0]
    Dq = D // nt
    members = np_ // E
    p = lax.axis_index("dp")
    t = lax.axis_index("tensor")
    nb, nc = D // dc, D // ec
    perq = Dq // ec

    def pair(src_g, src_l, i, q):
        slot = lax.rem(q, ns)
        cols = pl.ds(pl.multiple_of(i * cw, cw), cw)
        return (
            pltpu.make_async_copy(src_g.at[:, cols], gpool.at[slot], gsem.at[slot]),
            pltpu.make_async_copy(src_l.at[:, cols], lpool.at[slot], lsem.at[slot]),
        )

    def down_d(c):
        cols = pl.ds(pl.multiple_of(c * dc, dc), dc)
        return pltpu.make_async_copy(dd.at[:, cols], dpool.at[c], dsem.at[c])

    def quarter(c):
        return lax.rem(t + 1 + c // perq, nt)

    def down_e(c):
        start = quarter(c) * Dq + lax.rem(c, perq) * ec
        cols = pl.ds(pl.multiple_of(start, ec), ec)
        return pltpu.make_async_copy(ed.at[:, cols], epool.at[c], esem.at[c])

    def start_pair(src_g, src_l, i, q):
        for copy in pair(src_g, src_l, i, q):
            copy.start()

    barrier = pltpu.get_barrier_semaphore()

    def greet_dp(k, _):
        pl.semaphore_signal(
            barrier, inc=1, device_id=(lax.rem(p + k, np_), t), device_id_type=MESH
        )
        return 0

    lax.fori_loop(1, np_, greet_dp, 0)
    for j in range(1, nt):
        pl.semaphore_signal(
            barrier, inc=1, device_id=(p, lax.rem(t + j, nt)), device_id_type=MESH
        )

    first = min(ns, nd + ne)
    for q in range(min(first, nd)):
        start_pair(dg, dl, q, q)
    for c in range(nb):
        down_d(c).start()
    for q in range(nd, first):
        start_pair(eg, el, q - nd, q)

    hid = hidden[...].astype(F32)
    ag[p] = (hid * rms_scale(hid) * dgain[...]).astype(BF16)
    pl.semaphore_wait(barrier, np_ + nt - 2)

    def ag_copy(k, src):
        return pltpu.make_async_remote_copy(
            src_ref=ag.at[src], dst_ref=ag.at[src], send_sem=ag_s.at[k],
            recv_sem=ag_r.at[src], device_id=(lax.rem(p + k, np_), t), device_id_type=MESH,
        )

    def send_ag(k, _):
        ag_copy(k, p).start()
        return 0

    lax.fori_loop(1, np_, send_ag, 0)

    wide = 128
    col = lax.broadcasted_iota(jnp.int32, (B, wide), 1)
    col_e = lax.shift_right_logical(col, 3)
    col_s = col & 7
    at0 = jnp.where(ids[:, 0:1] == col_e, 1.0, 0.0).astype(F32)
    at1 = jnp.where(ids[:, 1:2] == col_e, 1.0, 0.0).astype(F32)
    named = at0 + at1
    r_i = lax.broadcasted_iota(jnp.int32, (B, B), 0)
    c_i = lax.broadcasted_iota(jnp.int32, (B, B), 1)
    lower = jnp.where(c_i < r_i, 1.0, 0.0).astype(BF16)
    before = jnp.dot(lower, named.astype(BF16), preferred_element_type=F32)
    spread = jnp.where(before.astype(jnp.int32) == col_s, named, 0.0)
    weighted = spread * (at0 * route[:, 0:1] + at1 * route[:, 1:2])

    sc = rms_scale(shortcut[...].astype(F32))
    mine = pl.ds(pl.multiple_of(t * Dq, Dq), Dq)
    moe_q = (shortcut[:, mine].astype(F32) * sc * mgain[:, mine]).astype(BF16)
    spread_t = jnp.transpose(spread)[: E * CP].astype(BF16)
    buf = jnp.dot(spread_t, moe_q, preferred_element_type=F32)
    disp[...] = buf.reshape(E, CP, Dq).astype(BF16)

    def di_copy(k, src):
        to = lax.rem(p + k, np_)
        return pltpu.make_async_remote_copy(
            src_ref=disp.at[to // members], dst_ref=land.at[t, src], send_sem=di_s.at[k],
            recv_sem=di_r.at[src], device_id=(to, t), device_id_type=MESH,
        )

    def send_di(k, _):
        di_copy(k, p).start()
        return 0

    lax.fori_loop(1, np_, send_di, 0)
    land[t, p] = disp[p // members]

    def recv_ag(k, _):
        ag_copy(k, lax.rem(p + k, np_)).wait_recv()
        return 0

    lax.fori_loop(1, np_, recv_ag, 0)
    for s in range(np_):
        stage[s * h : (s + 1) * h, :] = ag[s].astype(F32)
    xd[...] = stage[...].astype(BF16)

    def dense_step(q, _):
        for copy in pair(dg, dl, q, q):
            copy.wait()
        slot = lax.rem(q, ns)
        cols = pl.ds(pl.multiple_of(q * cw, cw), cw)
        inner_d[:, cols] = gated(xd[...], gpool[slot], lpool[slot])
        later = q + ns - nd

        @pl.when(later < ne)
        def _():
            start_pair(eg, el, later, q + ns)

        return 0

    def rl_copy(j, src):
        return pltpu.make_async_remote_copy(
            src_ref=land.at[src], dst_ref=land.at[src], send_sem=rl_s.at[j],
            recv_sem=rl_r.at[src], device_id=(p, lax.rem(t + j, nt)), device_id_type=MESH,
        )

    half = nd // 2
    lax.fori_loop(0, half, dense_step, 0)

    def recv_di(k, _):
        di_copy(k, lax.rem(p + k, np_)).wait_recv()
        return 0

    lax.fori_loop(1, np_, recv_di, 0)
    for j in range(1, nt):
        rl_copy(j, t).start()
    lax.fori_loop(half, nd, dense_step, 0)

    def dense_down_step(c, _):
        down_d(c).wait()
        o = jnp.dot(inner_d[...], dpool[c], preferred_element_type=F32)
        cols = pl.ds(pl.multiple_of(c * dc, dc), dc)
        for s in range(np_):
            ds[s, :, cols] = o[s * h : (s + 1) * h, :].astype(BF16)
        return 0

    lax.fori_loop(0, nb, dense_down_step, 0)

    def ds_copy(k, src):
        to = lax.rem(p + k, np_)
        return pltpu.make_async_remote_copy(
            src_ref=ds.at[to], dst_ref=dland.at[src], send_sem=ds_s.at[k],
            recv_sem=ds_r.at[src], device_id=(to, t), device_id_type=MESH,
        )

    def send_ds(k, _):
        ds_copy(k, p).start()
        return 0

    lax.fori_loop(1, np_, send_ds, 0)

    for j in range(1, nt):
        rl_copy(j, lax.rem(t + j, nt)).wait_recv()
    for q in range(nt):
        xe[:, q * Dq : (q + 1) * Dq] = land[q].astype(F32).reshape(np_ * CP, Dq).astype(BF16)

    def expert_step(i, _):
        q = i + nd
        for copy in pair(eg, el, i, q):
            copy.wait()
        slot = lax.rem(q, ns)
        cols = pl.ds(pl.multiple_of(i * cw, cw), cw)
        inner_e[:, cols] = gated(xe[...], gpool[slot], lpool[slot])

        @pl.when(i + ns < ne)
        def _():
            start_pair(eg, el, i + ns, q + ns)

        return 0

    tail = min(max(ne - ns, 0), ne)
    lax.fori_loop(0, tail, expert_step, 0)
    for c in range(nc):
        down_e(c).start()
    lax.fori_loop(tail, ne, expert_step, 0)

    def rs_copy(j, to, src):
        return pltpu.make_async_remote_copy(
            src_ref=rs.at[to], dst_ref=rsland.at[src], send_sem=rs_s.at[j],
            recv_sem=rs_r.at[src], device_id=(p, lax.rem(t + j, nt)), device_id_type=MESH,
        )

    def expert_down_step(c, _):
        down_e(c).wait()
        o = jnp.dot(inner_e[...], epool[c], preferred_element_type=F32)
        cols = pl.ds(pl.multiple_of(lax.rem(c, perq) * ec, ec), ec)
        rs[quarter(c), :, :, cols] = o.reshape(np_, CP, ec).astype(BF16)
        j = c // perq + 1

        @pl.when((lax.rem(c, perq) == perq - 1) & (j < nt))
        def _():
            rs_copy(j, lax.rem(t + j, nt), t).start()

        return 0

    lax.fori_loop(0, nc, expert_down_step, 0)

    total = rs[t].astype(F32)
    for j in range(1, nt):
        src = lax.rem(t + j, nt)
        rs_copy(j, src, src).wait_recv()
        total = total + rsland[src].astype(F32)
    ret[...] = total.astype(BF16)

    def re_copy(k, src):
        to = lax.rem(p + k, np_)
        return pltpu.make_async_remote_copy(
            src_ref=ret.at[to], dst_ref=retland.at[src], send_sem=re_s.at[k],
            recv_sem=re_r.at[src], device_id=(to, t), device_id_type=MESH,
        )

    def send_re(k, _):
        re_copy(k, p).start()
        return 0

    lax.fori_loop(1, np_, send_re, 0)
    retland[p] = ret[p]

    dland[p] = ds[p]

    def recv_ds(k, _):
        ds_copy(k, lax.rem(p + k, np_)).wait_recv()
        return 0

    lax.fori_loop(1, np_, recv_ds, 0)
    acc = hid
    for s in range(np_):
        acc = acc + dland[s].astype(F32)

    def recv_re(k, _):
        re_copy(k, lax.rem(p + k, np_)).wait_recv()
        return 0

    lax.fori_loop(1, np_, recv_re, 0)
    summed = jnp.sum(retland[...].astype(F32).reshape(E, members, CP, Dq), axis=1)
    moe = jnp.dot(
        weighted[:, : E * CP], summed.reshape(E * CP, Dq),
        precision=lax.Precision.HIGHEST, preferred_element_type=F32,
    )
    for q in range(nt):
        fin[q] = moe[q * h : (q + 1) * h, :]

    def fi_copy(j, src):
        to = lax.rem(t + j, nt)
        return pltpu.make_async_remote_copy(
            src_ref=fin.at[to], dst_ref=finland.at[src], send_sem=fi_s.at[j],
            recv_sem=fi_r.at[src], device_id=(p, to), device_id_type=MESH,
        )

    for j in range(1, nt):
        fi_copy(j, t).start()
    finland[t] = fin[t]
    for j in range(1, nt):
        fi_copy(j, lax.rem(t + j, nt)).wait_recv()
    for q in range(nt):
        cols = slice(q * Dq, (q + 1) * Dq)
        out[:, cols] = (acc[:, cols] + finland[q]).astype(BF16)

    def sent(k, _):
        ag_copy(k, p).wait_send()
        di_copy(k, p).wait_send()
        ds_copy(k, p).wait_send()
        re_copy(k, p).wait_send()
        return 0

    lax.fori_loop(1, np_, sent, 0)
    for j in range(1, nt):
        rl_copy(j, t).wait_send()
        rs_copy(j, lax.rem(t + j, nt), t).wait_send()
        fi_copy(j, t).wait_send()


def local(np_, nt, hidden, shortcut, ids, route, dgain, mgain, dg, dl, dd, eg, el, ed):
    h, D = hidden.shape
    Dq = D // nt
    fd, fe = dg.shape[1], eg.shape[1]
    cw = min(256, fd, fe)
    nd, ne = fd // cw, fe // cw
    ns = min(6, nd + ne)
    dc, ec = min(1024, D), min(512, Dq)
    cfg = (np_, nt, cw, ns, nd, ne, dc, ec)
    dma = pltpu.SemaphoreType.DMA
    vm = pltpu.VMEM
    vspec = pl.BlockSpec(memory_space=pltpu.VMEM)
    aspec = pl.BlockSpec(memory_space=pl.ANY)
    return pl.pallas_call(
        functools.partial(kernel, cfg),
        out_shape=jax.ShapeDtypeStruct((h, D), BF16),
        in_specs=[vspec] * 6 + [aspec] * 6,
        out_specs=vspec,
        scratch_shapes=[
            vm((ns, D, cw), BF16), vm((ns, D, cw), BF16),
            vm((D // dc, fd, dc), BF16), vm((D // ec, fe, ec), BF16),
            vm((np_, h, D), BF16), vm((np_ * h, D), F32), vm((np_ * h, D), BF16),
            vm((np_ * h, fd), BF16), vm((np_, h, D), BF16), vm((np_, h, D), BF16),
            vm((E, CP, Dq), BF16), vm((nt, np_, CP, Dq), BF16), vm((np_ * CP, D), BF16),
            vm((np_ * CP, fe), BF16), vm((nt, np_, CP, Dq), BF16), vm((nt, np_, CP, Dq), BF16),
            vm((np_, CP, Dq), BF16), vm((np_, CP, Dq), BF16),
            vm((nt, h, Dq), F32), vm((nt, h, Dq), F32),
            dma((ns,)), dma((ns,)), dma((D // dc,)), dma((D // ec,)),
            dma((np_,)), dma((np_,)), dma((np_,)), dma((np_,)),
            dma((nt,)), dma((nt,)), dma((np_,)), dma((np_,)),
            dma((nt,)), dma((nt,)), dma((np_,)), dma((np_,)),
            dma((nt,)), dma((nt,)),
        ],
        compiler_params=pltpu.CompilerParams(
            collective_id=0, has_side_effects=True, vmem_limit_bytes=64 * 1024 * 1024 - 65536
        ),
    )(hidden, shortcut, ids, route, dgain.reshape(1, D), mgain.reshape(1, D), dg, dl, dd, eg, el, ed)


def solution(mesh):
    in_specs = (
        P(("dp", "tensor"), None),
        P("dp", None),
        P("dp", None),
        P("dp", None),
        P(),
        P(),
        P(None, "dp"),
        P(None, "dp"),
        P("dp", None),
        P(None, ("dp", "tensor")),
        P(None, ("dp", "tensor")),
        P(("dp", "tensor"), None),
    )
    body = functools.partial(local, mesh.shape["dp"], mesh.shape["tensor"])
    return jax.shard_map(
        body, mesh=mesh, in_specs=in_specs, out_specs=P(("dp", "tensor"), None), check_vma=False
    )
```

time: 216 us -> 51.4 us (0.24)
  waiting for transfers between devices: 104 us -> 0 us
  Pallas kernels: 0 us -> 47.1 us
  matrix products: 39.2 us -> 0 us
  blocking collectives: 36 us -> 0 us
  between operations: 14.8 us -> 0.01 us
  starting transfers between devices: 10.9 us -> 0 us
  other arithmetic: 6.21 us -> 0 us
    unnamed x4 -> x0, waiting for transfers between devices: 104 us -> none
    pallas_call x0 -> x1, Pallas kernels: none -> 47.1 us  [local(): pl.pallas_call(functools.partial(kernel, cfg), out_shape=jax.ShapeDtypeSt...]
    dot_general x6 -> x0, matrix products: 39.2 us -> none  [the longest x1 13.7 us: local(): jnp.dot(inner, expert_down, preferred_element_type=jnp.float32)]
    all_gather x1 -> x0, blocking collectives: 36 us -> none  [local(): piece = lax.all_gather(normed, 'dp', axis=0, tiled=True)]
    all_to_all x2 -> x0, starting transfers between devices: 10.8 us -> none  [the longest x1 7.31 us: local(): lax.all_to_all(outgoing, 'dp', split_axis=0, concat_axis=0, tiled=True)]
    reduce_sum x4 -> x0, other arithmetic: 2.9 us -> none  [the longest x2 1.95 us: normalize(): jnp.mean(values * values, axis=-1, keepdims=True) + EPSILON]
  transfers between devices with their start and end apart: 4 -> 0, of which waited for: 3 -> 0; matrix products, arithmetic and copies ran while one was open for 9% -> 0% of each run, Pallas kernels for 0% -> 0%
where the time goes in v1:
time: 51.4 us; the launch traced here: 51.2 us
  Pallas kernels  47.1 us (92%)
  local copies, waits for them, and re-layouts  4.08 us (8%)
    pallas_call x1, Pallas kernels, local(): pl.pallas_call(functools.partial(kernel, cfg), out_shape=jax.ShapeDtypeSt...  47.1 us
    unnamed x3, local copies, waits for them, and re-layouts  4.08 us

profile of v1, /device:TPU:0, one launch (start us, length us, event | category | flops | bytes accessed | tf_op | source)
XLA Modules:
  0.0 51.2 jit_solution(10454954748279445544)
XLA Ops:
  0.0 1.4 %copy.13.ids = s32[16,2]{1,0:T(8,128)} copy(s32[16,2]{0,1:T(2,128)} %param.14) | data formatting | bytes 256 | tf_op args[2]
  1.4 1.3 %copy.14.route = f32[16,2]{1,0:T(8,128)} copy(f32[16,2]{0,1:T(2,128)} %param.15) | data formatting | bytes 256 | tf_op args[3]
  2.7 47.1 %shard_map.118 = bf16[4,4096]{1,0:T(4,128)(2,1)} custom-call(bf16[4,4096]{1,0:T(4,128)(2,1)} %hidden.1, bf16[16,4096]{1,0:T(8,128)(2,1)} %shortcut.1, s32[16,2]{1,0:T(8,128)} %copy.13.ids, f32[16,2]{1,0:T(8,128)} %copy.14.route, f32[1,4096]{1,0:T(1,128)} %bitcast.2, f32[1,4096]{1,0:T(1,128)} %bitcast.3, bf16[4096,1024]{1,0:T(8,128)(2,1)} %dg.1, ...), custom_call_target="tpu_custom_call" | custom-call | tf_op jit(solution)/shard_map/pallas_call | solution.py:345
  49.8 1.4 %copy.16 = bf16[4,4096]{1,0:T(4,128)(2,1)} copy(bf16[4,4096]{1,0:T(4,128)(2,1)} %shard_map.118) | data formatting | bytes 65536
